TPU v7x, 32 devices: a whole 2x2x4 slice. The times are simulated.
32 devices in a mesh: seq: 4 (over y, x), mem: 8 (over z, core).
Axes of the slice: x: 2, y: 2, z: 4, core: 2. Of those that a mesh axis runs over, the one named last changes fastest.
Arguments:
- hidden: bfloat16 [8192, 2048], P(('seq', 'mem')), may hold values from -6 to 6
- routes: int32 [8192, 2], P(('seq', 'mem')), may hold values from 0 to 7, all different within a row; in each aligned block of 256 rows (0 to 255, 256 to 511, ...) at most 64 rows name the same one
- gate_levels: int32 [8192, 2], P(('seq', 'mem')), may hold values from 1 to 255
- query_weight: bfloat16 [2048, 1024], P('seq'), may hold values from -0.125 to 0.125
- key_weight: bfloat16 [8, 2048, 1024], P('mem', 'seq'), may hold values from -0.125 to 0.125
- value_weight: bfloat16 [8, 2048, 1024], P('mem', 'seq'), may hold values from -0.125 to 0.125
Outputs:
- mixed: bfloat16 [8192, 1024], P(('seq', 'mem'))
Inputs may be any that keep to these rules, and one draw needn't show every extreme that they name: `routes`: the two memories of a row differ. In the rows of one device no memory is named by more than 64 rows, a bound that some block reaches.
All inputs are finite; a program needn't handle non-finite values.
Results may differ from a plain program's by a relative error of at most 0.01.
Values may be sent and summed in bfloat16 or wider, within the bound.
No kernel may reach another device: no remote copies, remote signals or barrier semaphores. Data moves between devices by JAX's collectives and lax.ppermute only.
A program may use at most 128 MiB of HBM per device.

v0:
```python
import jax
import jax.numpy as jnp
from jax import lax
from jax.sharding import PartitionSpec as P

HEADS = 8
DK = 128
BLOCK = 512
CAP = 64


def entering(array, axis, join, neutral):
    place = lax.axis_index(axis)
    gathered = lax.all_gather(array.astype(jnp.bfloat16), axis)
    state = jnp.zeros_like(array) + jnp.asarray(neutral, array.dtype)

    def one(step, state):
        return join(state, lax.dynamic_index_in_dim(gathered, step, 0, False).astype(array.dtype))

    return lax.fori_loop(0, place, one, state)


def add_states(earlier, later):
    return earlier + later


def on_device(hidden, routes, gate_levels, query_weight, key_weight, value_weight):
    count = hidden.shape[0]
    model = hidden.shape[1]
    width = query_weight.shape[1]
    mem_local = key_weight.shape[0]
    experts = mem_local * lax.axis_size("mem")
    highest = lax.Precision.HIGHEST
    onehot = (routes[:, :, None] == jnp.arange(experts, dtype=jnp.int32)[None, None, :]).astype(
        jnp.int32
    )
    per_token = jnp.sum(onehot, axis=1)
    before = jnp.cumsum(per_token, axis=0) - per_token
    place = jnp.sum(onehot * before[:, None, :], axis=2)
    slots = (routes * CAP + place).reshape(-1)
    owner_of = jnp.arange(2 * count, dtype=jnp.int32) // 2
    match = jnp.arange(experts * CAP, dtype=jnp.int32)[:, None] == slots[None, :]
    source = jnp.sum(jnp.where(match, owner_of[None, :], 0), axis=1)
    filled = jnp.any(match, axis=1)
    sent_rows = jnp.where(
        filled[:, None], jnp.take(hidden, source, axis=0), jnp.zeros((), hidden.dtype)
    )
    sent_rows = sent_rows.reshape(experts, CAP, model)
    columns = hidden
    queries = jnp.dot(
        columns,
        lax.all_gather(query_weight, "seq", axis=0, tiled=True),
        preferred_element_type=jnp.float32,
    ).astype(jnp.bfloat16)
    sent_queries = jnp.where(
        filled[:, None], jnp.take(queries, source, axis=0), jnp.zeros((), queries.dtype)
    )
    sent_queries = sent_queries.reshape(experts, CAP, width)
    arrived, arrived_queries = (
        lax.all_to_all(sent_rows, "mem", split_axis=0, concat_axis=1, tiled=True),
        lax.all_to_all(sent_queries, "mem", split_axis=0, concat_axis=1, tiled=True),
    )
    length = arrived.shape[1]
    columns = arrived
    key_part = jnp.einsum(
        "mrc,mch->mrh",
        columns,
        lax.all_gather(key_weight, "seq", axis=1, tiled=True),
        preferred_element_type=jnp.float32,
    )
    value_part = jnp.einsum(
        "mrc,mch->mrh",
        columns,
        lax.all_gather(value_weight, "seq", axis=1, tiled=True),
        preferred_element_type=jnp.float32,
    )
    keys = key_part
    values = value_part
    keys = keys.astype(jnp.bfloat16)
    values = values.astype(jnp.bfloat16)
    nblocks = length // BLOCK
    shape5 = (mem_local, nblocks, BLOCK, HEADS, DK)
    q_five = arrived_queries.reshape(shape5)
    k_five = keys.reshape(shape5)
    v_five = values.reshape(shape5)
    block_states = jnp.einsum(
        "mnkhd,mnkhe->mnhde", k_five, v_five, preferred_element_type=jnp.float32
    )
    within = jnp.cumsum(block_states, axis=1) - block_states
    local_total = jnp.sum(block_states, axis=1)
    nothing = jnp.zeros_like(local_total)
    incoming = entering(local_total, "seq", add_states, nothing)
    states = (incoming[:, None] + within).reshape(mem_local * nblocks, HEADS, DK, DK)
    flat = (mem_local * nblocks, BLOCK, HEADS, DK)
    rowids = jnp.arange(BLOCK, dtype=jnp.int32)
    causal = (rowids[:, None] >= rowids[None, :]).astype(jnp.float32)

    def attend(inputs):
        q_block, k_block, v_block, state = inputs
        scores = (
            jnp.einsum("qhd,khd->hqk", q_block, k_block, preferred_element_type=jnp.float32)
            * causal[None]
        )
        local = jnp.einsum("hqk,khd->qhd", scores, v_block.astype(jnp.float32), precision=highest)
        carried = jnp.einsum("qhd,hde->qhe", q_block.astype(jnp.float32), state, precision=highest)
        reads = local + carried
        scale = lax.rsqrt(jnp.mean(reads * reads, axis=-1, keepdims=True) + 1e-06)
        return (reads * scale).astype(jnp.bfloat16)

    normed = lax.map(
        attend, (q_five.reshape(flat), k_five.reshape(flat), v_five.reshape(flat), states)
    )
    normed = normed.reshape(mem_local, length, width)
    returned = lax.all_to_all(normed, "mem", split_axis=1, concat_axis=0, tiled=True)
    returned = returned.reshape(experts * CAP, width)
    picked = jnp.take(returned, slots, axis=0).reshape(count, 2, width)
    levels = gate_levels.astype(jnp.float32)
    gates = levels / jnp.sum(levels, axis=1, keepdims=True)
    mixed = jnp.sum(gates[:, :, None] * picked.astype(jnp.float32), axis=1)
    return mixed.astype(jnp.bfloat16)


def solution(mesh):
    return jax.shard_map(
        on_device,
        mesh=mesh,
        in_specs=(
            P(("seq", "mem"), None),
            P(("seq", "mem"), None),
            P(("seq", "mem"), None),
            P("seq", None),
            P("mem", "seq", None),
            P("mem", "seq", None),
        ),
        out_specs=P(("seq", "mem"), None),
        check_vma=False,
    )
```

profile of v0, /device:TPU:0, one launch (start us, length us, event | category | flops | bytes accessed | tf_op | source)
XLA Modules:
  0.0 289.7 jit_solution(13704537950358973058)
XLA Ops:
  6.5 0.7 all-gather.10.cloned.1.call-update
  7.3 0.7 all-gather.6.cloned.1.call-update
  8.1 0.7 all-gather.8.cloned.1.call-update
  8.8 0.6 reduce-window.6
  9.4 0.2 slice_reduce_fusion
  9.9 0.1 reshape.211
  10.1 0.2 fusion.24
  10.3 0.2 select_reduce_fusion
  10.6 2.5 gather_fusion
  13.1 0.3 select_select_fusion
  13.5 55.2 %all_to_all.12 = bf16[8,64,2048]{2,1,0:T(8,128)(2,1)S(1)} all-to-all(bf16[8,64,2048]{2,1,0:T(8,128)(2,1)S(1)} %select_select_fusion), channel_id=1, replica_groups=mesh['seq'=4,'mem'=8] {'mem'}, dimensions={0} | all-to-all | bytes 4194304 | tf_op jit(solution)/shard_map/all_to_all | solution.py:60
  68.7 1.4 copy-done.4
  70.0 5.5 %fusion.15 = bf16[512,1024]{1,0:T(8,128)(2,1)} fusion(bf16[512,2048]{1,0:T(8,128)(2,1)S(1)} %bitcast.80, bf16[1,2048,1024]{2,1,0:T(8,128)(2,1)} %all-gather.10.cloned.1.call-done), kind=kOutput, calls=%fused_computation.20 | convolution fusion | flops 2148007936 | bytes 7340032 | tf_op jit(solution)/shard_map/mrc,mch->mrh/dot_general | solution.py:65
  75.5 1.6 copy.74
  77.1 41.9 %all-gather.6.cloned.1.call-done = bf16[1,2048,1024]{2,1,0:T(8,128)(2,1)} async-done(((bf16[1,512,1024]{2,1,0:T(8,128)(2,1)}), bf16[1,2048,1024]{2,1,0:T(8,128)(2,1)}) %all-gather.6.cloned.1.call-update) | async-done | bytes 4194320 | tf_op jit(solution)/shard_map/all_gather | solution.py:74
  119.0 5.2 %fusion.18 = bf16[64,8,8,128]{3,2,1,0:T(8,128)(2,1)S(1)} fusion(bf16[512,2048]{1,0:T(8,128)(2,1)} %bitcast.81, bf16[1,2048,1024]{2,1,0:T(8,128)(2,1)} %all-gather.6.cloned.1.call-done), kind=kOutput, calls=%fused_computation.21 | convolution fusion | flops 2148007936 | bytes 7340032 | tf_op jit(solution)/shard_map/mrc,mch->mrh/dot_general | solution.py:71
  124.2 1.0 copy-done.2
  125.2 1.2 fusion.36
  126.3 47.1 %all-gather.8.cloned.1.call-done = bf16[2048,1024]{1,0:T(8,128)(2,1)} async-done(((bf16[512,1024]{1,0:T(8,128)(2,1)}), bf16[2048,1024]{1,0:T(8,128)(2,1)}) %all-gather.8.cloned.1.call-update) | async-done | bytes 4194320 | tf_op jit(solution)/shard_map/all_gather | solution.py:52
  173.5 3.4 %convolution_convert_fusion = bf16[256,1024]{1,0:T(8,128)(2,1)S(1)} fusion(bf16[256,2048]{1,0:T(8,128)(2,1)S(1)} %copy-done, bf16[2048,1024]{1,0:T(8,128)(2,1)} %all-gather.8.cloned.1.call-done), kind=kOutput, calls=%fused_computation.22 | convolution fusion | flops 1074003968 | bytes 5767168 | tf_op jit(solution)/shard_map/dot_general | solution.py:50
  176.9 2.8 gather_fusion.1
  179.7 2.4 select_select_fusion.1
  182.1 4.6 %all-to-all-start.1 = ((bf16[8,64,1024]{2,1,0:T(8,128)(2,1)}), bf16[8,64,1024]{2,1,0:T(8,128)(2,1)}, u32[]{:S(2)}, u32[]{:S(2)}) async-start(bf16[8,64,1024]{2,1,0:T(8,128)(2,1)} %select_select_fusion.1), calls=%async_computation.1 | async-start | bytes 2097152 | tf_op jit(solution)/shard_map/all_to_all | solution.py:61
  186.7 1.1 fusion.25
  187.8 13.9 %all-gather.12.cloned.1.call-done = bf16[32,128,128]{2,1,0:T(8,128)(2,1)} async-done(((bf16[8,128,128]{2,1,0:T(8,128)(2,1)}), bf16[32,128,128]{2,1,0:T(8,128)(2,1)}) %all-gather.12.cloned.1.call-update) | async-done | bytes 1048592 | tf_op jit(solution)/shard_map/all_gather | solution.py:14
  201.7 0.2 while.2
  201.9 11.5 %all-to-all-done.1 = bf16[8,64,1024]{2,1,0:T(8,128)(2,1)} async-done(((bf16[8,64,1024]{2,1,0:T(8,128)(2,1)}), bf16[8,64,1024]{2,1,0:T(8,128)(2,1)}, u32[]{:S(2)}, u32[]{:S(2)}) %all-to-all-start.1) | async-done | bytes 1048608 | tf_op jit(solution)/shard_map/all_to_all | solution.py:61
  213.4 1.5 copy.76
  214.9 1.2 fusion.30
  216.2 1.1 fusion.28
  217.2 0.1 copy-done.1
  217.4 0.3 copy-done.3
  217.7 5.5 %fusion.7 = (f32[512,8]{0,1:T(8,128)S(1)}, f32[8,128,512]{2,1,0:T(8,128)S(1)}) fusion(f32[8,128,512]{2,1,0:T(8,128)S(1)} %fusion.28, f32[8,512,512]{2,1,0:T(8,128)S(1)} %fusion.30, f32[512,512]{1,0:T(8,128)S(1)} %copy-done.1, bf16[64,8,8,128]{3,2,1,0:T(8,128)(2,1)S(1)} %copy-done.3), kind=kOutput, calls=%fused_computation.13 | convolution fusion | flops 3224891392 | bytes 14696448 | tf_op jit(solution)/shard_map/while/body/eval_jaxpr/hqk,khd->qhd/dot_general | solution.py:104
  223.2 1.3 fusion.8
  224.5 4.7 %copy.70 = bf16[1,512,1024]{2,0,1:T(2,128)(2,1)S(1)} copy(bf16[1,512,1024]{1,2,0:T(8,128)(2,1)} %bitcast.78) | data formatting | bytes 2097152 | tf_op jit(solution)/shard_map/reshape | solution.py:113
  229.2 0.5 broadcast.156
  229.8 7.8 %reduce.2 = bf16[512,1024]{1,0:T(8,128)(2,1)} reduce(bf16[512,1,1024]{2,1,0:T(2,128)(2,1)S(1)} %bitcast.77, bf16[]{:T(256)} %broadcast.156), dimensions={1}, to_apply=%bitcast.55.reduce_sub_computation | reduce | bytes 2097154
  237.5 2.6 reshape.245
  240.2 3.6 %all-to-all-start.2 = ((bf16[8,2,32768]{2,1,0:T(2,128)(2,1)}), bf16[8,2,32768]{2,1,0:T(2,128)(2,1)S(1)}, u32[]{:S(2)}, u32[]{:S(2)}) async-start(bf16[8,2,32768]{2,1,0:T(2,128)(2,1)} %reshape.245), calls=%async_computation.2 | async-start | bytes 2097152 | tf_op jit(solution)/shard_map/all_to_all | solution.py:114
  243.7 0.1 reshape.217
  243.9 0.2 copy.60
  244.1 0.1 copy.59
  244.3 26.0 %all-to-all-done.2 = bf16[8,2,32768]{2,1,0:T(2,128)(2,1)S(1)} async-done(((bf16[8,2,32768]{2,1,0:T(2,128)(2,1)}), bf16[8,2,32768]{2,1,0:T(2,128)(2,1)S(1)}, u32[]{:S(2)}, u32[]{:S(2)}) %all-to-all-start.2) | async-done | bytes 1048608 | tf_op jit(solution)/shard_map/all_to_all | solution.py:114
  270.2 3.5 %reshape.246 = bf16[512,1,1024]{2,1,0:T(2,128)(2,1)} reshape(bf16[8,2,32768]{2,1,0:T(2,128)(2,1)S(1)} %all-to-all-done.2) | data formatting | bytes 2097152
  273.7 2.0 copy.94
  275.6 2.1 gather_fusion.2
  277.7 0.4 gather.23
  278.2 5.0 %multiply_reduce_fusion = bf16[256,1024]{1,0:T(8,128)(2,1)} fusion(bf16[256,2,1024]{2,1,0:T(2,128)(2,1)S(1)} %gather.23, pred[256,2]{1,0:T(8,128)(4,1)S(1)} %copy.60, f32[256,2]{1,0:T(8,128)S(1)} %copy.59), kind=kLoop, calls=%fused_computation.15 | loop fusion | flops 1835008 | bytes 1575424 | tf_op jit(solution)/shard_map/reduce_sum | solution.py:119
  (35 shorter events, 0.7 us)
Async XLA Ops:
  6.5 4.1 %copy-start = (bf16[256,2048]{1,0:T(8,128)(2,1)S(1)}, bf16[256,2048]{1,0:T(8,128)(2,1)}, u32[]{:S(2)}) copy-start(bf16[256,2048]{1,0:T(8,128)(2,1)} %param.8) | copy-start | bytes 3145732
  6.5 2.3 copy-start.5
  6.5 62.1 %all-gather.10.cloned.1.call-start = ((), (), s32[]{:S(2)}) async-start(), calls=%async_computation.5 | async-start | bytes 5242880 | tf_op jit(solution)/shard_map/all_gather | solution.py:68
  7.3 111.8 %all-gather.6.cloned.1.call-start = ((), (), s32[]{:S(2)}) async-start(), calls=%async_computation.3 | async-start | bytes 5242880 | tf_op jit(solution)/shard_map/all_gather | solution.py:74
  8.0 165.5 %all-gather.8.cloned.1.call-start = ((), (), s32[]{:S(2)}) async-start(), calls=%async_computation.4 | async-start | bytes 5242880 | tf_op jit(solution)/shard_map/all_gather | solution.py:52
  8.7 193.0 %all-gather.12.cloned.1.call-start = ((), (), s32[]{:S(2)}) async-start(), calls=%async_computation.6 | async-start | bytes 1310720 | tf_op jit(solution)/shard_map/all_gather | solution.py:14
  68.7 1.4 copy-start.4
  124.2 1.0 copy-start.2
  182.1 31.3 %all-to-all-start.1 = ((bf16[8,64,1024]{2,1,0:T(8,128)(2,1)}), bf16[8,64,1024]{2,1,0:T(8,128)(2,1)}, u32[]{:S(2)}, u32[]{:S(2)}) async-start(bf16[8,64,1024]{2,1,0:T(8,128)(2,1)} %select_select_fusion.1), calls=%async_computation.1 | async-start | bytes 2097152 | tf_op jit(solution)/shard_map/all_to_all | solution.py:61
  216.1 1.2 copy-start.1
  216.2 1.5 copy-start.3
  237.5 6.5 %copy-start.6 = (s32[256,2]{0,1:T(2,128)S(1)}, s32[256,2]{0,1:T(2,128)}, u32[]{:S(2)}) copy-start(s32[256,2]{0,1:T(2,128)} %param.10) | copy-start | bytes 6148
  240.2 30.1 %all-to-all-start.2 = ((bf16[8,2,32768]{2,1,0:T(2,128)(2,1)}), bf16[8,2,32768]{2,1,0:T(2,128)(2,1)S(1)}, u32[]{:S(2)}, u32[]{:S(2)}) async-start(bf16[8,2,32768]{2,1,0:T(2,128)(2,1)} %reshape.245), calls=%async_computation.2 | async-start | bytes 2097152 | tf_op jit(solution)/shard_map/all_to_all | solution.py:114
Sparse Core Ops, SparseCore 0:
  9.2 55.3 all-gather.9
  66.4 52.5 all-gather.5
  120.9 52.5 all-gather.7
  175.2 26.4 all-gather.11
where the time goes:
time: 290 us
  waiting for transfers between devices  142 us (49%)
  blocking collectives  55.2 us (19%)
  local copies, waits for them, and re-layouts  28.1 us (10%)
  matrix products  23 us (8%)
  other arithmetic  19.1 us (7%)
  between operations  13.4 us (5%)
  starting transfers between devices  8.28 us (3%)
    all_to_all x1, blocking collectives, on_device(): lax.all_to_all(sent_rows, 'mem', split_axis=0, concat_axis=1, tiled=True)  55.2 us
    all_gather x1, waiting for transfers between devices, on_device(): lax.all_gather(query_weight, 'seq', axis=0, tiled=True)  47.1 us
    all_gather x1, waiting for transfers between devices, on_device(): lax.all_gather(value_weight, 'seq', axis=1, tiled=True)  41.9 us
    all_to_all x1, waiting for transfers between devices, on_device(): lax.all_to_all(normed, 'mem', split_axis=1, concat_axis=0, tiled=True)  26 us
    all_gather x1, waiting for transfers between devices, entering(): gathered = lax.all_gather(array.astype(jnp.bfloat16), axis)  13.9 us
    unnamed x19, local copies, waits for them, and re-layouts  12.9 us
    all_to_all x1, waiting for transfers between devices, on_device(): lax.all_to_all(sent_queries, 'mem', split_axis=0, concat_axis=1, tiled=True)  11.5 us
    unnamed x1, other arithmetic  7.77 us
  transfers between devices with their start and end apart: 6, of which 5 were waited for; matrix products, arithmetic and copies ran while one was open for 10% of the time, Pallas kernels for 0%

commit v1 on v0

--- a/solution.py
+++ b/solution.py
@@ -49,7 +49,9 @@
     columns = hidden
     queries = jnp.dot(
         columns,
-        lax.all_gather(query_weight, "seq", axis=0, tiled=True),
+        jnp.concatenate(
+            lax.all_to_all(jnp.stack([query_weight] * lax.axis_size("seq")), "seq", 0, 0), axis=0
+        ),
         preferred_element_type=jnp.float32,
     ).astype(jnp.bfloat16)
     sent_queries = jnp.where(

time: 290 us -> 267 us (0.921)
  blocking collectives: 55.2 us -> 0 us
  waiting for transfers between devices: 142 us -> 154 us
  starting transfers between devices: 8.28 us -> 19.6 us
  matrix products: 23 us -> 30.7 us
    all_to_all x0 -> x2, waiting for transfers between devices: none -> 99.3 us  [the longest x1 56.9 us: on_device(): lax.all_to_all(jnp.stack([query_weight] * lax.axis_size('seq')), 'seq', 0...]
    all_to_all x1 -> x0, blocking collectives: 55.2 us -> none  [on_device(): lax.all_to_all(sent_rows, 'mem', split_axis=0, concat_axis=1, tiled=True)]
    all_gather x1 -> x0, waiting for transfers between devices: 47.1 us -> none  [on_device(): lax.all_gather(query_weight, 'seq', axis=0, tiled=True)]
    all_gather x1, waiting for transfers between devices: 41.9 us -> 7.32 us  [on_device(): lax.all_gather(value_weight, 'seq', axis=1, tiled=True)]
    all_to_all x0 -> x2, starting transfers between devices: none -> 11.4 us  [the longest x1 6.04 us: on_device(): lax.all_to_all(sent_rows, 'mem', split_axis=0, concat_axis=1, tiled=True)]
    all_to_all x1, waiting for transfers between devices: 11.5 us -> 3.62 us  [on_device(): lax.all_to_all(sent_queries, 'mem', split_axis=0, concat_axis=1, tiled=True)]
    another operation x1 -> x2, local copies, waits for them, and re-layouts: 0.01 us -> 3.73 us  [the longest x1 3.73 us: on_device(): jnp.stack([query_weight] * lax.axis_size('seq'))]
    dot_general x1, matrix products: 5.49 us -> 8.89 us  [attend(): jnp.einsum('hqk,khd->qhd', scores, v_block.astype(jnp.float32), precision...]
  transfers between devices with their start and end apart: 6 -> 7, of which waited for: 5 -> 6; matrix products, arithmetic and copies ran while one was open for 10% -> 14% of each run, Pallas kernels for 0% -> 0%
where the time goes in v1:
time: 267 us; the launch traced here: 266 us
  waiting for transfers between devices  154 us (58%)
  matrix products  30.7 us (11%)
  local copies, waits for them, and re-layouts  29.3 us (11%)
  starting transfers between devices  19.6 us (7%)
  other arithmetic  19.2 us (7%)
  between operations  13.4 us (5%)
    all_to_all x1, waiting for transfers between devices, on_device(): lax.all_to_all(jnp.stack([query_weight] * lax.axis_size('seq')), 'seq', 0...  56.9 us
    all_to_all x1, waiting for transfers between devices, on_device(): lax.all_to_all(sent_rows, 'mem', split_axis=0, concat_axis=1, tiled=True)  42.4 us
    all_to_all x1, waiting for transfers between devices, on_device(): lax.all_to_all(normed, 'mem', split_axis=1, concat_axis=0, tiled=True)  26 us
    all_gather x1, waiting for transfers between devices, entering(): gathered = lax.all_gather(array.astype(jnp.bfloat16), axis)  16.2 us
    unnamed x23, local copies, waits for them, and re-layouts  11.1 us
    dot_general x1, matrix products, attend(): jnp.einsum('hqk,khd->qhd', scores, v_block.astype(jnp.float32), precision...  8.89 us
    unnamed x1, other arithmetic  7.77 us
    all_gather x1, waiting for transfers between devices, on_device(): lax.all_gather(value_weight, 'seq', axis=1, tiled=True)  7.32 us
  transfers between devices with their start and end apart: 7, of which 6 were waited for; matrix products, arithmetic and copies ran while one was open for 14% of the time, Pallas kernels for 0%

profile of v1, /device:TPU:0, one launch (start us, length us, event | category | flops | bytes accessed | tf_op | source)
XLA Modules:
  0.0 266.3 jit_solution(10081660174100360475)
XLA Ops:
  6.5 0.7 all-gather.7.cloned.1.call-update
  7.3 3.7 %stack.2 = bf16[4,512,1024]{2,1,0:T(8,128)(2,1)} broadcast(bf16[512,1024]{1,0:T(8,128)(2,1)} %param.11), dimensions={1,2} | broadcast | bytes 5242880 | tf_op jit(solution)/shard_map/stack | solution.py:53
  11.0 5.3 %all-to-all-start.1 = ((bf16[4,512,1024]{2,1,0:T(8,128)(2,1)}), bf16[4,512,1024]{2,1,0:T(8,128)(2,1)}, u32[]{:S(2)}, u32[]{:S(2)}) async-start(bf16[4,512,1024]{2,1,0:T(8,128)(2,1)} %stack.2), calls=%async_computation.1 | async-start | bytes 8388608 | tf_op jit(solution)/shard_map/all_to_all | solution.py:53
  16.3 0.7 all-gather.5.cloned.1.call-update
  17.1 0.6 reduce-window.6
  17.7 0.2 slice_reduce_fusion
  18.2 0.1 reshape.216
  18.3 0.2 select_reduce_fusion
  18.6 0.2 fusion.24
  18.9 2.5 gather_fusion
  21.4 1.7 select_select_fusion
  23.1 56.9 %all-to-all-done.1 = bf16[4,512,1024]{2,1,0:T(8,128)(2,1)} async-done(((bf16[4,512,1024]{2,1,0:T(8,128)(2,1)}), bf16[4,512,1024]{2,1,0:T(8,128)(2,1)}, u32[]{:S(2)}, u32[]{:S(2)}) %all-to-all-start.1) | async-done | bytes 4194336 | tf_op jit(solution)/shard_map/all_to_all | solution.py:53
  79.9 6.0 %all-to-all-start = ((bf16[8,64,2048]{2,1,0:T(8,128)(2,1)}), bf16[8,64,2048]{2,1,0:T(8,128)(2,1)}, u32[]{:S(2)}, u32[]{:S(2)}) async-start(bf16[8,64,2048]{2,1,0:T(8,128)(2,1)} %select_select_fusion), calls=%async_computation | async-start | bytes 4194304 | tf_op jit(solution)/shard_map/all_to_all | solution.py:62
  86.0 3.4 %convolution_convert_fusion = bf16[256,1024]{1,0:T(8,128)(2,1)S(1)} fusion(bf16[256,2048]{1,0:T(8,128)(2,1)S(1)} %copy-done, bf16[2048,1024]{1,0:T(8,128)(2,1)} %bitcast.10), kind=kOutput, calls=%fused_computation.22 | convolution fusion | flops 1074003968 | bytes 5767168 | tf_op jit(solution)/shard_map/dot_general | solution.py:50
  89.4 2.1 gather_fusion.1
  91.5 1.2 select_select_fusion.1
  92.7 42.4 %all-to-all-done = bf16[8,64,2048]{2,1,0:T(8,128)(2,1)} async-done(((bf16[8,64,2048]{2,1,0:T(8,128)(2,1)}), bf16[8,64,2048]{2,1,0:T(8,128)(2,1)}, u32[]{:S(2)}, u32[]{:S(2)}) %all-to-all-start) | async-done | bytes 2097184 | tf_op jit(solution)/shard_map/all_to_all | solution.py:62
  135.1 3.6 %all-to-all-start.2 = ((bf16[8,64,1024]{2,1,0:T(8,128)(2,1)}), bf16[8,64,1024]{2,1,0:T(8,128)(2,1)S(1)}, u32[]{:S(2)}, u32[]{:S(2)}) async-start(bf16[8,64,1024]{2,1,0:T(8,128)(2,1)} %select_select_fusion.1), calls=%async_computation.2 | async-start | bytes 2097152 | tf_op jit(solution)/shard_map/all_to_all | solution.py:63
  138.8 6.2 %fusion.15 = bf16[512,1024]{1,0:T(8,128)(2,1)} fusion(bf16[512,2048]{1,0:T(8,128)(2,1)} %bitcast.8, bf16[1,2048,1024]{2,1,0:T(8,128)(2,1)} %all-gather.7.cloned.1.call-done), kind=kOutput, calls=%fused_computation.20 | convolution fusion | flops 2148007936 | bytes 7340032 | tf_op jit(solution)/shard_map/mrc,mch->mrh/dot_general | solution.py:67
  145.0 1.5 copy.74
  146.5 7.3 %all-gather.5.cloned.1.call-done = bf16[1,2048,1024]{2,1,0:T(8,128)(2,1)} async-done(((bf16[1,512,1024]{2,1,0:T(8,128)(2,1)}), bf16[1,2048,1024]{2,1,0:T(8,128)(2,1)}) %all-gather.5.cloned.1.call-update) | async-done | bytes 4194320 | tf_op jit(solution)/shard_map/all_gather | solution.py:76
  153.8 5.2 %fusion.18 = bf16[64,8,8,128]{3,2,1,0:T(8,128)(2,1)S(1)} fusion(bf16[512,2048]{1,0:T(8,128)(2,1)} %bitcast.8, bf16[1,2048,1024]{2,1,0:T(8,128)(2,1)} %all-gather.5.cloned.1.call-done), kind=kOutput, calls=%fused_computation.21 | convolution fusion | flops 2148007936 | bytes 7340032 | tf_op jit(solution)/shard_map/mrc,mch->mrh/dot_general | solution.py:73
  159.0 1.4 fusion.36
  160.5 1.1 fusion.25
  161.6 3.6 %all-to-all-done.2 = bf16[8,64,1024]{2,1,0:T(8,128)(2,1)S(1)} async-done(((bf16[8,64,1024]{2,1,0:T(8,128)(2,1)}), bf16[8,64,1024]{2,1,0:T(8,128)(2,1)S(1)}, u32[]{:S(2)}, u32[]{:S(2)}) %all-to-all-start.2) | async-done | bytes 1048608 | tf_op jit(solution)/shard_map/all_to_all | solution.py:63
  165.2 0.3 copy.76
  165.5 0.9 copy-done.2
  166.4 4.5 %fusion.30 = f32[8,512,512]{2,1,0:T(8,128)} fusion(bf16[512,8,128]{0,2,1:T(8,128)(2,1)S(1)} %bitcast.75, bf16[512,8,128]{2,1,0:T(8,128)(2,1)S(1)} %bitcast.72), kind=kOutput, calls=%fused_computation.37 | convolution fusion | flops 536870912 | bytes 10485760 | tf_op jit(solution)/shard_map/while/body/eval_jaxpr/qhd,khd->hqk/dot_general | solution.py:103
  170.9 16.2 %all-gather.9.cloned.1.call-done = bf16[32,128,128]{2,1,0:T(8,128)(2,1)} async-done(((bf16[8,128,128]{2,1,0:T(8,128)(2,1)}), bf16[32,128,128]{2,1,0:T(8,128)(2,1)}) %all-gather.9.cloned.1.call-update) | async-done | bytes 1048592 | tf_op jit(solution)/shard_map/all_gather | solution.py:14
  187.2 0.2 while.2
  187.4 0.8 copy-done.6
  188.2 1.1 fusion.28
  189.3 0.2 copy-done.3
  189.4 0.3 copy-done.5
  189.7 8.9 %fusion.7 = (f32[512,8]{0,1:T(8,128)S(1)}, f32[8,128,512]{2,1,0:T(8,128)S(1)}) fusion(f32[8,128,512]{2,1,0:T(8,128)S(1)} %fusion.28, f32[8,512,512]{2,1,0:T(8,128)} %fusion.30, f32[512,512]{1,0:T(8,128)S(1)} %copy-done.3, bf16[64,8,8,128]{3,2,1,0:T(8,128)(2,1)S(1)} %copy-done.5), kind=kOutput, calls=%fused_computation.13 | convolution fusion | flops 3224891392 | bytes 14696448 | tf_op jit(solution)/shard_map/while/body/eval_jaxpr/hqk,khd->qhd/dot_general | solution.py:106
  198.6 1.3 fusion.8
  199.9 4.7 %copy.70 = bf16[1,512,1024]{2,0,1:T(2,128)(2,1)S(1)} copy(bf16[1,512,1024]{1,2,0:T(8,128)(2,1)} %bitcast.79) | data formatting | bytes 2097152 | tf_op jit(solution)/shard_map/reshape | solution.py:115
  204.7 0.5 broadcast.158
  205.2 7.8 %reduce.2 = bf16[512,1024]{1,0:T(8,128)(2,1)} reduce(bf16[512,1,1024]{2,1,0:T(2,128)(2,1)S(1)} %bitcast.78, bf16[]{:T(256)} %broadcast.158), dimensions={1}, to_apply=%bitcast.56.reduce_sub_computation | reduce | bytes 2097154
  213.0 2.6 reshape.251
  215.6 4.6 %all-to-all-start.3 = ((bf16[8,2,32768]{2,1,0:T(2,128)(2,1)}), bf16[8,2,32768]{2,1,0:T(2,128)(2,1)S(1)}, u32[]{:S(2)}, u32[]{:S(2)}) async-start(bf16[8,2,32768]{2,1,0:T(2,128)(2,1)} %reshape.251), calls=%async_computation.3 | async-start | bytes 2097152 | tf_op jit(solution)/shard_map/all_to_all | solution.py:116
  220.4 0.2 copy.60
  220.8 26.0 %all-to-all-done.3 = bf16[8,2,32768]{2,1,0:T(2,128)(2,1)S(1)} async-done(((bf16[8,2,32768]{2,1,0:T(2,128)(2,1)}), bf16[8,2,32768]{2,1,0:T(2,128)(2,1)S(1)}, u32[]{:S(2)}, u32[]{:S(2)}) %all-to-all-start.3) | async-done | bytes 1048608 | tf_op jit(solution)/shard_map/all_to_all | solution.py:116
  246.8 3.5 %reshape.252 = bf16[512,1,1024]{2,1,0:T(2,128)(2,1)} reshape(bf16[8,2,32768]{2,1,0:T(2,128)(2,1)S(1)} %all-to-all-done.3) | data formatting | bytes 2097152
  250.2 2.0 copy.94
  252.2 2.1 gather_fusion.2
  254.3 0.4 gather.23
  254.7 5.0 %multiply_reduce_fusion = bf16[256,1024]{1,0:T(8,128)(2,1)} fusion(bf16[256,2,1024]{2,1,0:T(2,128)(2,1)S(1)} %gather.23, pred[256,2]{1,0:T(8,128)(4,1)S(1)} %copy.60, f32[256,2]{1,0:T(8,128)S(1)} %copy.59), kind=kLoop, calls=%fused_computation.15 | loop fusion | flops 1835008 | bytes 1575424 | tf_op jit(solution)/shard_map/reduce_sum | solution.py:121
  (40 shorter events, 0.9 us)
Async XLA Ops:
  6.5 12.4 %copy-start = (bf16[256,2048]{1,0:T(8,128)(2,1)S(1)}, bf16[256,2048]{1,0:T(8,128)(2,1)}, u32[]{:S(2)}) copy-start(bf16[256,2048]{1,0:T(8,128)(2,1)} %param.8) | copy-start | bytes 3145732
  6.5 132.2 %all-gather.7.cloned.1.call-start = ((), (), s32[]{:S(2)}) async-start(), calls=%async_computation.5 | async-start | bytes 5242880 | tf_op jit(solution)/shard_map/all_gather | solution.py:70
  11.0 6.1 %copy-start.7 = (s32[256,2]{0,1:T(2,128)S(1)}, s32[256,2]{0,1:T(2,128)}, u32[]{:S(2)}) copy-start(s32[256,2]{0,1:T(2,128)} %param.9) | copy-start | bytes 6148
  11.0 69.0 %all-to-all-start.1 = ((bf16[4,512,1024]{2,1,0:T(8,128)(2,1)}), bf16[4,512,1024]{2,1,0:T(8,128)(2,1)}, u32[]{:S(2)}, u32[]{:S(2)}) async-start(bf16[4,512,1024]{2,1,0:T(8,128)(2,1)} %stack.2), calls=%async_computation.1 | async-start | bytes 8388608 | tf_op jit(solution)/shard_map/all_to_all | solution.py:53
  16.3 137.5 %all-gather.5.cloned.1.call-start = ((), (), s32[]{:S(2)}) async-start(), calls=%async_computation.4 | async-start | bytes 5242880 | tf_op jit(solution)/shard_map/all_gather | solution.py:76
  79.9 55.2 %all-to-all-start = ((bf16[8,64,2048]{2,1,0:T(8,128)(2,1)}), bf16[8,64,2048]{2,1,0:T(8,128)(2,1)}, u32[]{:S(2)}, u32[]{:S(2)}) async-start(bf16[8,64,2048]{2,1,0:T(8,128)(2,1)} %select_select_fusion), calls=%async_computation | async-start | bytes 4194304 | tf_op jit(solution)/shard_map/all_to_all | solution.py:62
  135.1 30.1 %all-to-all-start.2 = ((bf16[8,64,1024]{2,1,0:T(8,128)(2,1)}), bf16[8,64,1024]{2,1,0:T(8,128)(2,1)S(1)}, u32[]{:S(2)}, u32[]{:S(2)}) async-start(bf16[8,64,1024]{2,1,0:T(8,128)(2,1)} %select_select_fusion.1), calls=%async_computation.2 | async-start | bytes 2097152 | tf_op jit(solution)/shard_map/all_to_all | solution.py:63
  138.7 48.4 %all-gather.9.cloned.1.call-start = ((), (), s32[]{:S(2)}) async-start(), calls=%async_computation.6 | async-start | bytes 1310720 | tf_op jit(solution)/shard_map/all_gather | solution.py:14
  146.5 12.5 %copy-start.1 = (bf16[512,1024]{0,1:T(8,128)(2,1)}, bf16[512,1024]{0,1:T(8,128)(2,1)S(1)}, u32[]{:S(2)}) copy-start(bf16[512,1024]{0,1:T(8,128)(2,1)S(1)} %copy.74) | copy-start | bytes 3145732
  159.0 1.4 copy-start.4
  165.2 1.2 copy-start.2
  187.1 1.0 copy-start.6
  188.2 1.2 copy-start.3
  188.2 1.5 copy-start.5
  213.0 7.6 %copy-start.8 = (s32[256,2]{0,1:T(2,128)S(1)}, s32[256,2]{0,1:T(2,128)}, u32[]{:S(2)}) copy-start(s32[256,2]{0,1:T(2,128)} %param.10) | copy-start | bytes 6148
  215.6 31.2 %all-to-all-start.3 = ((bf16[8,2,32768]{2,1,0:T(2,128)(2,1)}), bf16[8,2,32768]{2,1,0:T(2,128)(2,1)S(1)}, u32[]{:S(2)}, u32[]{:S(2)}) async-start(bf16[8,2,32768]{2,1,0:T(2,128)(2,1)} %reshape.251), calls=%async_computation.3 | async-start | bytes 2097152 | tf_op jit(solution)/shard_map/all_to_all | solution.py:116
Sparse Core Ops, SparseCore 0:
  9.2 89.5 all-gather.6
  100.6 53.1 all-gather.4
  160.6 26.4 all-gather.8
